TPU v7x, 32 devices: a whole 2x2x4 slice. The times are simulated.
32 devices in a mesh: dom: 8 (over y, x, core), sub: 4 (over z).
Axes of the slice: x: 2, y: 2, z: 4, core: 2. Of those that a mesh axis runs over, the one named last changes fastest.
Arguments:
- features: bfloat16 [32768, 602], P(('dom', 'sub')), may hold values from -6 to 6
- w_inner: bfloat16 [602, 256], replicated, may hold values from -0.25 to 0.25
- bias_inner: float32 [256], replicated, may hold values from -6 to 6
- w_outer: bfloat16 [256, 41], replicated, may hold values from -0.375 to 0.375
- bias_outer: float32 [41], replicated, may hold values from -6 to 6
- tiles: bfloat16 [256, 32, 128, 128], P(('dom', 'sub')), may hold values from -3 to 3
- tile_col: int32 [256, 32], P(('dom', 'sub')), may hold values from 0 to 39, as said below
- degrees: int32 [32768], P(('dom', 'sub')), may hold values from 1 to 32
- send_rows: int32 [32, 32, 128], P(('dom', 'sub')), may hold values from -1 to 1023, as said below
Outputs:
- logits: float32 [32768, 41], P(('dom', 'sub'))
Inputs may be any that keep to these rules, and one draw needn't show every extreme that they name: send_rows[e, p, s] is the row, among device e's 1024 vertices, that fills slot s of e's list for device p, or -1 for an unused slot; live slots come first and every list has 1 to 128 live slots; every sender has a full list, and in every draw some device receives full lists from all senders. tile_col[d * 8 + r, t] is the column block, in device d's column space, of tile t of row block r; the 32 column blocks of a row block are distinct.
All inputs are finite; a program needn't handle non-finite values.
Results may differ from a plain program's by a relative error of at most 0.0042.
Values may be sent and summed in bfloat16 or wider, within the bound.
A program may use at most 128 MiB of HBM per device.

v0:
```python
import jax
import jax.numpy as jnp
from jax import lax
from jax.sharding import PartitionSpec as P


def deliver_inner(outgoing):
    return lax.all_to_all(outgoing, ("dom", "sub"), split_axis=0, concat_axis=0, tiled=True)


def deliver_outer(outgoing):
    return lax.all_to_all(outgoing, ("dom", "sub"), split_axis=0, concat_axis=0, tiled=True)


def aggregate(feature_rows, tiles, tile_col, send_lists, deliver):
    block_rows = tiles.shape[2]
    width = feature_rows.shape[1]
    clipped = jnp.clip(send_lists, 0, feature_rows.shape[0] - 1)
    live_slot = (send_lists >= 0)[:, :, None]
    outgoing = jnp.where(
        live_slot, jnp.take(feature_rows, clipped, axis=0), jnp.zeros((), feature_rows.dtype)
    )
    arrived = deliver(outgoing)
    columns = jnp.concatenate([feature_rows.reshape(-1, block_rows, width), arrived], axis=0)

    def rowblock(element):
        tile_set, col_set = element
        blocks = columns[col_set]
        return jnp.einsum("tij,tjw->iw", tile_set, blocks, preferred_element_type=jnp.float32)

    summed = lax.map(rowblock, (tiles, tile_col))
    return summed.reshape(feature_rows.shape[0], width)


def on_device(
    features, w_inner, bias_inner, w_outer, bias_outer, tiles, tile_col, degrees, send_rows
):
    send_lists = send_rows[0]
    classes = w_outer.shape[1]
    padded_width = 128 * ((classes + 127) // 128)
    inv_sqrt = lax.rsqrt(degrees.astype(jnp.float32))[:, None]
    projected = (jnp.dot(features, w_inner, preferred_element_type=jnp.float32) * inv_sqrt).astype(
        jnp.bfloat16
    )
    agg_inner = aggregate(projected, tiles, tile_col, send_lists, deliver_inner)
    hidden = (inv_sqrt * jax.nn.relu(inv_sqrt * agg_inner + bias_inner)).astype(jnp.bfloat16)
    w_padded = jnp.pad(w_outer, ((0, 0), (0, padded_width - classes)))
    scores = jnp.dot(hidden, w_padded, preferred_element_type=jnp.float32).astype(jnp.bfloat16)
    agg_outer = aggregate(scores, tiles, tile_col, send_lists, deliver_outer)
    return inv_sqrt * agg_outer[:, :classes] + bias_outer


def solution(mesh):
    return jax.shard_map(
        on_device,
        mesh=mesh,
        in_specs=(
            P(("dom", "sub"), None),
            P(),
            P(),
            P(),
            P(),
            P(("dom", "sub"), None, None, None),
            P(("dom", "sub"), None),
            P(("dom", "sub")),
            P(("dom", "sub"), None, None),
        ),
        out_specs=P(("dom", "sub"), None),
        check_vma=False,
    )
```

profile of v0, /device:TPU:0, one launch (start us, length us, event | category | flops | bytes accessed | tf_op | source)
XLA Modules:
  0.0 210.9 jit_solution(7271072908278238845)
XLA Ops:
  0.0 0.8 fusion.19
  3.0 1.6 fusion.12
  4.6 16.9 %gather_fusion.2 = bf16[4096,256]{1,0:T(8,128)(2,1)} fusion(bf16[1024,256]{1,0:T(8,128)(2,1)S(1)} %fusion.12, s32[4096]{0:T(1024)S(1)} %fusion.19), kind=kCustom, calls=%fused_computation.2 | custom fusion | bytes 4210688 | tf_op jit(solution)/shard_map/jit(_take)/gather | solution.py:21
  21.5 4.4 %select_select_fusion = bf16[32,128,256]{2,1,0:T(8,128)(2,1)} fusion(bf16[32,128,256]{2,1,0:T(8,128)(2,1)} %bitcast.87, pred[32,128]{1,0:T(8,128)(4,1)S(1)} %compare_and_fusion, pred[32,128]{1,0:T(8,128)(4,1)S(1)} %compare_bitcast_fusion), kind=kLoop, calls=%fused_computation.25 | loop fusion | flops 2097152 | bytes 4202496 | tf_op jit(solution)/shard_map/jit(_where)/select_n | solution.py:20
  25.9 7.5 %all-to-all-start = ((bf16[32,128,256]{2,1,0:T(8,128)(2,1)}), bf16[32,128,256]{2,1,0:T(8,128)(2,1)}, u32[]{:S(2)}, u32[]{:S(2)}) async-start(bf16[32,128,256]{2,1,0:T(8,128)(2,1)} %select_select_fusion), calls=%async_computation | async-start | bytes 4194304 | tf_op jit(solution)/shard_map/all_to_all | solution.py:8
  33.4 46.9 %all-to-all-done = bf16[32,128,256]{2,1,0:T(8,128)(2,1)} async-done(((bf16[32,128,256]{2,1,0:T(8,128)(2,1)}), bf16[32,128,256]{2,1,0:T(8,128)(2,1)}, u32[]{:S(2)}, u32[]{:S(2)}) %all-to-all-start) | async-done | bytes 2097184 | tf_op jit(solution)/shard_map/all_to_all | solution.py:8
  80.3 3.3 %pad_maximum_fusion = bf16[40,128,256]{2,1,0:T(8,128)(2,1)} fusion(bf16[32,128,256]{2,1,0:T(8,128)(2,1)} %all-to-all-done, bf16[8,128,256]{2,1,0:T(8,128)(2,1)S(1)} %bitcast.85), kind=kLoop, calls=%fused_computation.24 | loop fusion | flops 1310720 | bytes 5242880 | tf_op jit(solution)/shard_map/concatenate | solution.py:24
  83.6 43.7 %while.20 = (s32[]{:T(128)}, f32[8,128,256]{2,1,0:T(8,128)}, bf16[8,32,128,128]{3,2,1,0:T(8,128)(2,1)}, s32[8,32]{1,0:T(8,128)}, bf16[40,128,256]{2,1,0:T(8,128)(2,1)}, /*index=5*/s32[]{:T(128)}) while((s32[]{:T(128)}, f32[8,128,256]{2,1,0:T(8,128)}, bf16[8,32,128,128]{3,2,1,0:T(8,128)(2,1)}, s32[8,32]{1,0:T(8,128)}, ...), condition=%wide.region_1.2_spmd, body=%wide.region_0.1_spmd.sunk | while | flops 268436576 | bytes 7476809 | solution.py:31
  84.3 2.4 %gather_fusion = bf16[32,128,256]{2,1,0:T(8,128)(2,1)S(1)} fusion(bf16[40,128,256]{2,1,0:T(8,128)(2,1)} %get-tuple-element.159, s32[1024]{0:T(1024)S(1)} %pad_clamp_fusion.4), kind=kCustom, calls=%fused_computation.clone.1 | custom fusion | bytes 4194432 | tf_op jit(solution)/shard_map/while/body/eval_jaxpr/gather | solution.py:28
  86.7 2.3 %fusion.37 = f32[8,128,256]{2,1,0:T(8,128)} fusion(f32[8,128,256]{2,1,0:T(8,128)} %get-tuple-element.150, s32[]{:T(128)} %get-tuple-element.149, bf16[32,128,256]{2,1,0:T(8,128)(2,1)S(1)} %gather_fusion, bf16[8,32,128,128]{3,2,1,0:T(8,128)(2,1)} %get-tuple-element.157), kind=kOutput, calls=%fused_computation.5.clone.1 | convolution fusion | flops 268435456 | bytes 3277824 | tf_op jit(solution)/shard_map/while/body/eval_jaxpr/tij,tjw->iw/dot_general | solution.py:29
  89.8 2.4 %gather_fusion = bf16[32,128,256]{2,1,0:T(8,128)(2,1)S(1)} fusion(bf16[40,128,256]{2,1,0:T(8,128)(2,1)} %get-tuple-element.159, s32[1024]{0:T(1024)S(1)} %pad_clamp_fusion.4), kind=kCustom, calls=%fused_computation.clone.1 | custom fusion | bytes 4194432 | tf_op jit(solution)/shard_map/while/body/eval_jaxpr/gather | solution.py:28
  92.2 2.3 %fusion.37 = f32[8,128,256]{2,1,0:T(8,128)} fusion(f32[8,128,256]{2,1,0:T(8,128)} %get-tuple-element.150, s32[]{:T(128)} %get-tuple-element.149, bf16[32,128,256]{2,1,0:T(8,128)(2,1)S(1)} %gather_fusion, bf16[8,32,128,128]{3,2,1,0:T(8,128)(2,1)} %get-tuple-element.157), kind=kOutput, calls=%fused_computation.5.clone.1 | convolution fusion | flops 268435456 | bytes 3277824 | tf_op jit(solution)/shard_map/while/body/eval_jaxpr/tij,tjw->iw/dot_general | solution.py:29
  95.2 2.4 %gather_fusion = bf16[32,128,256]{2,1,0:T(8,128)(2,1)S(1)} fusion(bf16[40,128,256]{2,1,0:T(8,128)(2,1)} %get-tuple-element.159, s32[1024]{0:T(1024)S(1)} %pad_clamp_fusion.4), kind=kCustom, calls=%fused_computation.clone.1 | custom fusion | bytes 4194432 | tf_op jit(solution)/shard_map/while/body/eval_jaxpr/gather | solution.py:28
  97.7 2.3 %fusion.37 = f32[8,128,256]{2,1,0:T(8,128)} fusion(f32[8,128,256]{2,1,0:T(8,128)} %get-tuple-element.150, s32[]{:T(128)} %get-tuple-element.149, bf16[32,128,256]{2,1,0:T(8,128)(2,1)S(1)} %gather_fusion, bf16[8,32,128,128]{3,2,1,0:T(8,128)(2,1)} %get-tuple-element.157), kind=kOutput, calls=%fused_computation.5.clone.1 | convolution fusion | flops 268435456 | bytes 3277824 | tf_op jit(solution)/shard_map/while/body/eval_jaxpr/tij,tjw->iw/dot_general | solution.py:29
  100.7 2.4 %gather_fusion = bf16[32,128,256]{2,1,0:T(8,128)(2,1)S(1)} fusion(bf16[40,128,256]{2,1,0:T(8,128)(2,1)} %get-tuple-element.159, s32[1024]{0:T(1024)S(1)} %pad_clamp_fusion.4), kind=kCustom, calls=%fused_computation.clone.1 | custom fusion | bytes 4194432 | tf_op jit(solution)/shard_map/while/body/eval_jaxpr/gather | solution.py:28
  103.1 2.3 %fusion.37 = f32[8,128,256]{2,1,0:T(8,128)} fusion(f32[8,128,256]{2,1,0:T(8,128)} %get-tuple-element.150, s32[]{:T(128)} %get-tuple-element.149, bf16[32,128,256]{2,1,0:T(8,128)(2,1)S(1)} %gather_fusion, bf16[8,32,128,128]{3,2,1,0:T(8,128)(2,1)} %get-tuple-element.157), kind=kOutput, calls=%fused_computation.5.clone.1 | convolution fusion | flops 268435456 | bytes 3277824 | tf_op jit(solution)/shard_map/while/body/eval_jaxpr/tij,tjw->iw/dot_general | solution.py:29
  106.1 2.4 %gather_fusion = bf16[32,128,256]{2,1,0:T(8,128)(2,1)S(1)} fusion(bf16[40,128,256]{2,1,0:T(8,128)(2,1)} %get-tuple-element.159, s32[1024]{0:T(1024)S(1)} %pad_clamp_fusion.4), kind=kCustom, calls=%fused_computation.clone.1 | custom fusion | bytes 4194432 | tf_op jit(solution)/shard_map/while/body/eval_jaxpr/gather | solution.py:28
  108.5 2.3 %fusion.37 = f32[8,128,256]{2,1,0:T(8,128)} fusion(f32[8,128,256]{2,1,0:T(8,128)} %get-tuple-element.150, s32[]{:T(128)} %get-tuple-element.149, bf16[32,128,256]{2,1,0:T(8,128)(2,1)S(1)} %gather_fusion, bf16[8,32,128,128]{3,2,1,0:T(8,128)(2,1)} %get-tuple-element.157), kind=kOutput, calls=%fused_computation.5.clone.1 | convolution fusion | flops 268435456 | bytes 3277824 | tf_op jit(solution)/shard_map/while/body/eval_jaxpr/tij,tjw->iw/dot_general | solution.py:29
  111.6 2.4 %gather_fusion = bf16[32,128,256]{2,1,0:T(8,128)(2,1)S(1)} fusion(bf16[40,128,256]{2,1,0:T(8,128)(2,1)} %get-tuple-element.159, s32[1024]{0:T(1024)S(1)} %pad_clamp_fusion.4), kind=kCustom, calls=%fused_computation.clone.1 | custom fusion | bytes 4194432 | tf_op jit(solution)/shard_map/while/body/eval_jaxpr/gather | solution.py:28
  114.0 2.4 %fusion.37 = f32[8,128,256]{2,1,0:T(8,128)} fusion(f32[8,128,256]{2,1,0:T(8,128)} %get-tuple-element.150, s32[]{:T(128)} %get-tuple-element.149, bf16[32,128,256]{2,1,0:T(8,128)(2,1)S(1)} %gather_fusion, bf16[8,32,128,128]{3,2,1,0:T(8,128)(2,1)} %get-tuple-element.157), kind=kOutput, calls=%fused_computation.5.clone.1 | convolution fusion | flops 268435456 | bytes 3277824 | tf_op jit(solution)/shard_map/while/body/eval_jaxpr/tij,tjw->iw/dot_general | solution.py:29
  117.1 2.4 %gather_fusion = bf16[32,128,256]{2,1,0:T(8,128)(2,1)S(1)} fusion(bf16[40,128,256]{2,1,0:T(8,128)(2,1)} %get-tuple-element.159, s32[1024]{0:T(1024)S(1)} %pad_clamp_fusion.4), kind=kCustom, calls=%fused_computation.clone.1 | custom fusion | bytes 4194432 | tf_op jit(solution)/shard_map/while/body/eval_jaxpr/gather | solution.py:28
  119.5 2.3 %fusion.37 = f32[8,128,256]{2,1,0:T(8,128)} fusion(f32[8,128,256]{2,1,0:T(8,128)} %get-tuple-element.150, s32[]{:T(128)} %get-tuple-element.149, bf16[32,128,256]{2,1,0:T(8,128)(2,1)S(1)} %gather_fusion, bf16[8,32,128,128]{3,2,1,0:T(8,128)(2,1)} %get-tuple-element.157), kind=kOutput, calls=%fused_computation.5.clone.1 | convolution fusion | flops 268435456 | bytes 3277824 | tf_op jit(solution)/shard_map/while/body/eval_jaxpr/tij,tjw->iw/dot_general | solution.py:29
  122.5 2.4 %gather_fusion = bf16[32,128,256]{2,1,0:T(8,128)(2,1)S(1)} fusion(bf16[40,128,256]{2,1,0:T(8,128)(2,1)} %get-tuple-element.159, s32[1024]{0:T(1024)S(1)} %pad_clamp_fusion.4), kind=kCustom, calls=%fused_computation.clone.1 | custom fusion | bytes 4194432 | tf_op jit(solution)/shard_map/while/body/eval_jaxpr/gather | solution.py:28
  124.9 2.3 %fusion.37 = f32[8,128,256]{2,1,0:T(8,128)} fusion(f32[8,128,256]{2,1,0:T(8,128)} %get-tuple-element.150, s32[]{:T(128)} %get-tuple-element.149, bf16[32,128,256]{2,1,0:T(8,128)(2,1)S(1)} %gather_fusion, bf16[8,32,128,128]{3,2,1,0:T(8,128)(2,1)} %get-tuple-element.157), kind=kOutput, calls=%fused_computation.5.clone.1 | convolution fusion | flops 268435456 | bytes 3277824 | tf_op jit(solution)/shard_map/while/body/eval_jaxpr/tij,tjw->iw/dot_general | solution.py:29
  127.3 1.4 fusion.16
  129.0 12.1 %gather_fusion.3 = bf16[4096,128]{1,0:T(8,128)(2,1)S(1)} fusion(bf16[1024,128]{1,0:T(8,128)(2,1)S(1)} %convolution_convert_fusion, s32[4096]{0:T(1024)S(1)} %fusion.19), kind=kCustom, calls=%fused_computation.3 | custom fusion | bytes 2113536 | tf_op jit(solution)/shard_map/jit(_take)/gather | solution.py:21
  141.2 2.4 %select_select_fusion.1 = bf16[32,128,128]{2,1,0:T(8,128)(2,1)} fusion(bf16[32,128,128]{2,1,0:T(8,128)(2,1)S(1)} %bitcast.88, pred[32,128]{1,0:T(8,128)(4,1)S(1)} %compare_and_fusion, pred[32,128]{1,0:T(8,128)(4,1)S(1)} %compare_bitcast_fusion), kind=kLoop, calls=%fused_computation.35 | loop fusion | flops 1048576 | bytes 2105344 | tf_op jit(solution)/shard_map/jit(_where)/select_n | solution.py:20
  143.6 4.6 %all-to-all-start.1 = ((bf16[32,128,128]{2,1,0:T(8,128)(2,1)}), bf16[32,128,128]{2,1,0:T(8,128)(2,1)S(1)}, u32[]{:S(2)}, u32[]{:S(2)}) async-start(bf16[32,128,128]{2,1,0:T(8,128)(2,1)} %select_select_fusion.1), calls=%async_computation.1 | async-start | bytes 2097152 | tf_op jit(solution)/shard_map/all_to_all | solution.py:12
  148.2 24.9 %all-to-all-done.1 = bf16[32,128,128]{2,1,0:T(8,128)(2,1)S(1)} async-done(((bf16[32,128,128]{2,1,0:T(8,128)(2,1)}), bf16[32,128,128]{2,1,0:T(8,128)(2,1)S(1)}, u32[]{:S(2)}, u32[]{:S(2)}) %all-to-all-start.1) | async-done | bytes 1048608 | tf_op jit(solution)/shard_map/all_to_all | solution.py:12
  173.1 1.2 pad_maximum_fusion.1
  174.3 35.6 %while.21 = (s32[]{:T(128)}, f32[8,128,128]{2,1,0:T(8,128)S(1)}, bf16[8,32,128,128]{3,2,1,0:T(8,128)(2,1)}, s32[8,32]{1,0:T(8,128)}, bf16[40,128,128]{2,1,0:T(8,128)(2,1)}, /*index=5*/s32[]{:T(128)}) while((s32[]{:T(128)}, f32[8,128,128]{2,1,0:T(8,128)S(1)}, bf16[8,32,128,128]{3,2,1,0:T(8,128)(2,1)}, s32[8,32]{1,0:T(8,128)}, ...), condition=%wide.region_3.4_spmd, body=%wide.region_2.3_spmd.sunk | while | flops 134218848 | bytes 4265545 | solution.py:31
  175.0 2.1 gather_fusion.1
  177.1 1.7 fusion.41
  179.5 2.1 gather_fusion.1
  181.5 1.7 fusion.41
  183.9 2.1 gather_fusion.1
  186.0 1.7 fusion.41
  188.4 2.1 gather_fusion.1
  190.4 1.7 fusion.41
  192.8 2.1 gather_fusion.1
  194.9 1.7 fusion.41
  197.3 2.1 gather_fusion.1
  199.3 1.7 fusion.41
  201.7 2.1 gather_fusion.1
  203.8 1.7 fusion.41
  206.2 2.1 gather_fusion.1
  208.2 1.7 fusion.41
  210.1 0.8 multiply_add_fusion
  (47 shorter events, 13.9 us)
Async XLA Ops:
  0.0 3.0 %copy-start = (bf16[1024,602]{0,1:T(8,128)(2,1)S(1)}, bf16[1024,602]{0,1:T(8,128)(2,1)}, u32[]{:S(2)}) copy-start(bf16[1024,602]{0,1:T(8,128)(2,1)} %param.13) | copy-start | bytes 3698692
  25.9 54.3 %all-to-all-start = ((bf16[32,128,256]{2,1,0:T(8,128)(2,1)}), bf16[32,128,256]{2,1,0:T(8,128)(2,1)}, u32[]{:S(2)}, u32[]{:S(2)}) async-start(bf16[32,128,256]{2,1,0:T(8,128)(2,1)} %select_select_fusion), calls=%async_computation | async-start | bytes 4194304 | tf_op jit(solution)/shard_map/all_to_all | solution.py:8
  83.6 43.7 %copy-start.2 = (f32[256]{0:T(256)S(1)}, f32[256]{0:T(256)}, u32[]{:S(2)}) copy-start(f32[256]{0:T(256)} %param.15) | copy-start | bytes 3076
  83.6 45.2 %copy-start.1 = (bf16[256,41]{0,1:T(8,128)(2,1)S(1)}, bf16[256,41]{0,1:T(8,128)(2,1)}, u32[]{:S(2)}) copy-start(bf16[256,41]{0,1:T(8,128)(2,1)} %param.16) | copy-start | bytes 62980
  143.6 29.5 %all-to-all-start.1 = ((bf16[32,128,128]{2,1,0:T(8,128)(2,1)}), bf16[32,128,128]{2,1,0:T(8,128)(2,1)S(1)}, u32[]{:S(2)}, u32[]{:S(2)}) async-start(bf16[32,128,128]{2,1,0:T(8,128)(2,1)} %select_select_fusion.1), calls=%async_computation.1 | async-start | bytes 2097152 | tf_op jit(solution)/shard_map/all_to_all | solution.py:12
  174.3 35.8 %copy-start.3 = (f32[41]{0:T(128)S(1)}, f32[41]{0:T(128)}, u32[]{:S(2)}) copy-start(f32[41]{0:T(128)} %param.17) | copy-start | bytes 496
where the time goes:
time: 214 us; the launch traced here: 211 us
  waiting for transfers between devices  71.8 us (34%)
  local copies, waits for them, and re-layouts  65.1 us (30%)
  matrix products  33.7 us (16%)
  other arithmetic  27.8 us (13%)
  starting transfers between devices  12 us (6%)
    all_to_all x1, waiting for transfers between devices, deliver_inner(): lax.all_to_all(outgoing, ('dom', 'sub'), split_axis=0, concat_axis=0, til...  46.9 us
    gather x16, local copies, waits for them, and re-layouts, rowblock(): blocks = columns[col_set]  35.9 us
    dot_general x16, matrix products, rowblock(): jnp.einsum('tij,tjw->iw', tile_set, blocks, preferred_element_type=jnp.fl...  31.8 us
    gather x2, local copies, waits for them, and re-layouts, aggregate(): jnp.take(feature_rows, clipped, axis=0)  29.1 us
    all_to_all x1, waiting for transfers between devices, deliver_outer(): lax.all_to_all(outgoing, ('dom', 'sub'), split_axis=0, concat_axis=0, til...  24.9 us
    select_n x16, other arithmetic, rowblock(): blocks = columns[col_set]  11.1 us
    all_to_all x1, starting transfers between devices, deliver_inner(): lax.all_to_all(outgoing, ('dom', 'sub'), split_axis=0, concat_axis=0, til...  7.45 us
    select_n x2, other arithmetic, aggregate(): jnp.where(live_slot, jnp.take(feature_rows, clipped, axis=0), jnp.zeros((...  6.83 us
  transfers between devices with their start and end apart: 2, of which 2 were waited for; matrix products, arithmetic and copies ran while one was open for 0% of the time, Pallas kernels for 0%

commit v1 on v0

v1 whole, which is shorter than its diff:
```python
import functools

import jax
import jax.numpy as jnp
from jax import lax
from jax.experimental import pallas as pl
from jax.experimental.pallas import tpu as pltpu
from jax.sharding import PartitionSpec as P

MESH = pl.DeviceIdType.MESH
NT = (((1,), (1,)), ((), ()))


def kernel(
    n_dom, n_sub, ft, w_inner, bias, w_outer, degrees, lists, where_tile, tiles_hbm, out,
    proj, out_in, got_in, acc_in, w_pad, scores, out_sc, got_sc, acc_sc, tiles,
    tile_sem, send_in, recv_in, send_sc, recv_sc,
):
    dom, sub = lax.axis_index("dom"), lax.axis_index("sub")
    peers = n_dom * n_sub
    hid, verts = proj.shape
    rows, per_row, blk, _ = tiles.shape
    own = verts // blk
    classes = w_outer.shape[0]

    def flip(a):
        total, bit = 0, 1
        while bit < n_dom:
            total = total + lax.rem(lax.div(dom, bit) + lax.div(a, bit), 2) * bit
            bit *= 2
        return total

    def target(k):
        return flip(lax.div(k, n_sub)), lax.rem(sub + lax.rem(k, n_sub), n_sub)

    def source(k):
        return flip(lax.div(k, n_sub)) * n_sub + lax.rem(sub + n_sub - lax.rem(k, n_sub), n_sub)

    def copy(src, dst, sends, recvs, k):
        return pltpu.make_async_remote_copy(
            src_ref=src.at[k], dst_ref=dst.at[k], send_sem=sends.at[k], recv_sem=recvs.at[k],
            device_id=target(k), device_id_type=MESH,
        )

    barrier = pltpu.get_barrier_semaphore()

    @pl.loop(1, peers)
    def _(k):
        pl.semaphore_signal(barrier, inc=1, device_id=target(k), device_id_type=MESH)

    tile_copy = pltpu.make_async_copy(tiles_hbm, tiles, tile_sem)
    tile_copy.start()
    inv = lax.rsqrt(degrees[...].astype(jnp.float32))
    w_t = w_inner[...].T
    wide = 2 * blk
    for v in range(0, verts, wide):
        part = jnp.dot(w_t, ft[:, v:v + wide], preferred_element_type=jnp.float32)
        proj[:, v:v + wide] = (part * inv[:, v:v + wide]).astype(proj.dtype)
    pl.semaphore_wait(barrier, peers - 1)

    def pick(k, table):
        slot_rows = []
        for each in (k, k + 1):
            to_dom, to_sub = target(each)
            slot_rows.append(lists[pl.ds(to_dom * n_sub + to_sub, 1), :])
        slots = jnp.concatenate(slot_rows, axis=1)
        hot = lax.broadcasted_iota(jnp.int32, (verts, 2 * blk), 0) == slots
        hot = jnp.where(hot, 1.0, 0.0).astype(table.dtype)
        return jnp.dot(table[...], hot, preferred_element_type=jnp.float32).astype(table.dtype)

    def deliver(table, outgoing, got, sends, recvs):
        first = pick(0, table)
        got[0] = first[:, :blk]
        outgoing[1] = first[:, blk:]
        copy(outgoing, got, sends, recvs, 1).start()

        @pl.loop(1, peers // 2)
        def _(pair):
            k = 2 * pair
            picked = pick(k, table)
            outgoing[k] = picked[:, :blk]
            outgoing[k + 1] = picked[:, blk:]
            copy(outgoing, got, sends, recvs, k).start()
            copy(outgoing, got, sends, recvs, k + 1).start()

    def add(acc, block, c0, c1, fresh):
        def tile(r, c):
            t = where_tile[r, c]
            found = tiles[r, jnp.maximum(t, 0)]
            return jnp.where(t >= 0, found, jnp.zeros_like(found))

        for r in range(0, rows, 2):
            weights = jnp.concatenate(
                [jnp.concatenate([tile(r + q, c0), tile(r + q, c1)], axis=1) for q in range(2)],
                axis=0,
            )
            term = lax.dot_general(block, weights, NT, preferred_element_type=jnp.float32)
            span = slice(r * blk, (r + 2) * blk)
            acc[:, span] = term if fresh else acc[:, span] + term

    def aggregate(table, outgoing, got, sends, recvs, acc):
        for c in range(0, own, 2):
            add(acc, table[:, c * blk:(c + 2) * blk], c, c + 1, c == 0)

        def arrived(k):
            block = jnp.concatenate([got[k], got[k + 1]], axis=1)
            add(acc, block, own + source(k), own + source(k + 1), False)

        copy(outgoing, got, sends, recvs, 1).wait_recv()
        arrived(0)

        @pl.loop(1, peers // 2)
        def _(pair):
            k = 2 * pair
            copy(outgoing, got, sends, recvs, k).wait_recv()
            copy(outgoing, got, sends, recvs, k + 1).wait_recv()
            arrived(k)

    deliver(proj, out_in, got_in, send_in, recv_in)
    w_pad[...] = jnp.zeros_like(w_pad)
    w_pad[0:classes, :] = w_outer[...]
    bias_col = jnp.broadcast_to(bias[...], (blk, hid)).T
    tile_copy.wait()
    aggregate(proj, out_in, got_in, send_in, recv_in, acc_in)
    for v in range(0, verts, blk):
        span = slice(v, v + blk)
        scale = inv[:, span]
        hidden = scale * jnp.maximum(scale * acc_in[:, span] + bias_col, 0.0)
        scores[:, span] = jnp.dot(
            w_pad[...], hidden.astype(jnp.bfloat16), preferred_element_type=jnp.float32
        ).astype(scores.dtype)
    deliver(scores, out_sc, got_sc, send_sc, recv_sc)
    aggregate(scores, out_sc, got_sc, send_sc, recv_sc, acc_sc)
    out[...] = acc_sc[0:classes, :]

    @pl.loop(1, peers)
    def _(k):
        copy(out_in, got_in, send_in, recv_in, k).wait_send()
        copy(out_sc, got_sc, send_sc, recv_sc, k).wait_send()


def on_device(
    n_dom, n_sub,
    features, w_inner, bias_inner, w_outer, bias_outer, tiles, tile_col, degrees, send_rows
):
    peers = n_dom * n_sub
    verts, hid = features.shape[0], w_inner.shape[1]
    classes = w_outer.shape[1]
    padded = 16 * ((classes + 15) // 16)
    blk = tiles.shape[2]
    columns = verts // blk + peers
    order = jnp.arange(tiles.shape[1], dtype=jnp.int32)
    hit = tile_col[:, None, :] == jnp.arange(columns, dtype=jnp.int32)[None, :, None]
    where_tile = jnp.max(jnp.where(hit, order, -1), axis=2)
    vmem = pl.BlockSpec(memory_space=pltpu.VMEM)
    bf16, f32 = jnp.bfloat16, jnp.float32
    agg = pl.pallas_call(
        functools.partial(kernel, n_dom, n_sub),
        out_shape=jax.ShapeDtypeStruct((classes, verts), f32),
        in_specs=[vmem] * 6
        + [pl.BlockSpec(memory_space=pltpu.SMEM), pl.BlockSpec(memory_space=pl.ANY)],
        out_specs=vmem,
        scratch_shapes=[
            pltpu.VMEM((hid, verts), bf16),
            pltpu.VMEM((peers, hid, blk), bf16),
            pltpu.VMEM((peers, hid, blk), bf16),
            pltpu.VMEM((hid, verts), f32),
            pltpu.VMEM((padded, hid), bf16),
            pltpu.VMEM((padded, verts), bf16),
            pltpu.VMEM((peers, padded, blk), bf16),
            pltpu.VMEM((peers, padded, blk), bf16),
            pltpu.VMEM((padded, verts), f32),
            pltpu.VMEM(tiles.shape, bf16),
            pltpu.SemaphoreType.DMA,
            pltpu.SemaphoreType.DMA((peers,)),
            pltpu.SemaphoreType.DMA((peers,)),
            pltpu.SemaphoreType.DMA((peers,)),
            pltpu.SemaphoreType.DMA((peers,)),
        ],
        compiler_params=pltpu.CompilerParams(
            collective_id=0, has_side_effects=True, vmem_limit_bytes=56 * 1024 * 1024
        ),
    )(
        features.T, w_inner, bias_inner[None, :], w_outer.T, degrees[None, :], send_rows[0],
        where_tile, tiles,
    )
    inv_sqrt = lax.rsqrt(degrees.astype(f32))[:, None]
    return inv_sqrt * agg.T + bias_outer


def solution(mesh):
    return jax.shard_map(
        functools.partial(on_device, mesh.shape["dom"], mesh.shape["sub"]),
        mesh=mesh,
        in_specs=(
            P(("dom", "sub"), None),
            P(),
            P(),
            P(),
            P(),
            P(("dom", "sub"), None, None, None),
            P(("dom", "sub"), None),
            P(("dom", "sub")),
            P(("dom", "sub"), None, None),
        ),
        out_specs=P(("dom", "sub"), None),
        check_vma=False,
    )
```

time: 214 us -> 74.7 us (0.35); the launches traced: 211 us -> 74.5 us
  waiting for transfers between devices: 71.8 us -> 0 us
  Pallas kernels: 0 us -> 71.3 us
  local copies, waits for them, and re-layouts: 65.1 us -> 0.01 us
  matrix products: 33.7 us -> 0 us
  other arithmetic: 27.8 us -> 3.11 us
  starting transfers between devices: 12 us -> 0 us
    all_to_all x2 -> x0, waiting for transfers between devices: 71.8 us -> none  [the longest x1 46.9 us: deliver_inner(): lax.all_to_all(outgoing, ('dom', 'sub'), split_axis=0, concat_axis=0, til...]
    pallas_call x0 -> x1, Pallas kernels: none -> 71.3 us  [on_device(): pl.pallas_call(functools.partial(kernel, n_dom, n_sub), out_shape=jax.Sha...]
    gather x18 -> x0, local copies, waits for them, and re-layouts: 64.9 us -> none  [the longest x16 35.9 us: rowblock(): blocks = columns[col_set]]
    dot_general x18 -> x0, matrix products: 33.7 us -> none  [the longest x16 31.8 us: rowblock(): jnp.einsum('tij,tjw->iw', tile_set, blocks, preferred_element_type=jnp.fl...]
    select_n x18 -> x0, other arithmetic: 18 us -> none  [the longest x16 11.1 us: rowblock(): blocks = columns[col_set]]
    all_to_all x2 -> x0, starting transfers between devices: 12 us -> none  [the longest x1 7.45 us: deliver_inner(): lax.all_to_all(outgoing, ('dom', 'sub'), split_axis=0, concat_axis=0, til...]
    concatenate x2 -> x0, other arithmetic: 4.52 us -> none  [aggregate(): jnp.concatenate([feature_rows.reshape(-1, block_rows, width), arrived], a...]
  transfers between devices with their start and end apart: 2 -> 0, of which waited for: 2 -> 0; matrix products, arithmetic and copies ran while one was open for 0% -> 0% of each run, Pallas kernels for 0% -> 0%
where the time goes in v1:
time: 74.7 us; the launch traced here: 74.5 us
  Pallas kernels  71.3 us (95%)
  other arithmetic  3.11 us (4%)
    pallas_call x1, Pallas kernels, on_device(): pl.pallas_call(functools.partial(kernel, n_dom, n_sub), out_shape=jax.Sha...  71.3 us
    add x1, other arithmetic, on_device(): return inv_sqrt * agg.T + bias_outer  1.69 us

profile of v1, /device:TPU:0, one launch (start us, length us, event | category | flops | bytes accessed | tf_op | source)
XLA Modules:
  0.0 74.5 jit_solution(9598540684752644728)
XLA Ops:
  0.0 0.0 copy-start
  0.0 0.0 copy-start.1
  0.0 1.4 %select_reduce_fusion.where_tile = s32[8,40]{1,0:T(8,128)} fusion(s32[8,32]{1,0:T(8,128)} %param.15), kind=kLoop, calls=%fused_computation.1 | loop fusion | flops 30400 | bytes 2304 | tf_op jit(solution)/shard_map/reduce_max | solution.py:154
  1.4 71.3 %shard_map.91 = f32[41,1024]{1,0:T(8,128)} custom-call(bf16[602,1024]{1,0:T(8,128)(2,1)} %bitcast.7, bf16[602,256]{1,0:T(8,128)(2,1)} %w_inner.1, f32[1,256]{1,0:T(1,128)} %bitcast.11, bf16[41,256]{1,0:T(8,128)(2,1)} %bitcast.8, s32[1,1024]{1,0:T(1,128)} %bitcast.10, s32[32,128]{1,0:T(8,128)} %bitcast.9, s32[8,40]{1,0:T(8,128)} %select_reduce_fusion.where_tile, ...), custom_call_target="tpu_custom_call" | custom-call | tf_op jit(solution)/shard_map/pallas_call | solution.py:157
  72.8 0.0 copy-done
  72.8 0.0 copy-done.1
  72.8 1.7 %add_bitcast_fusion = f32[1024,41]{0,1:T(8,128)} fusion(f32[41,1024]{1,0:T(8,128)} %shard_map.91, f32[41]{0:T(128)S(1)} %copy-done.1, f32[1024]{0:T(1024)S(1)} %convert_rsqrt_fusion), kind=kLoop, calls=%fused_computation | loop fusion | flops 83968 | bytes 340132 | tf_op jit(solution)/shard_map/add | solution.py:188
  (1 shorter events, 0.0 us)
Async XLA Ops:
  0.0 72.8 %copy-start = (s32[1024]{0:T(1024)S(1)}, s32[1024]{0:T(1024)}, u32[]{:S(2)}) copy-start(s32[1024]{0:T(1024)} %param.16) | copy-start | bytes 12292
  0.0 72.8 %copy-start.1 = (f32[41]{0:T(128)S(1)}, f32[41]{0:T(128)}, u32[]{:S(2)}) copy-start(f32[41]{0:T(128)} %param.13) | copy-start | bytes 496

commit v2 on v1

--- a/solution.py
+++ b/solution.py
@@ -15,6 +15,7 @@
     n_dom, n_sub, ft, w_inner, bias, w_outer, degrees, lists, where_tile, tiles_hbm, out,
     proj, out_in, got_in, acc_in, w_pad, scores, out_sc, got_sc, acc_sc, tiles,
     tile_sem, send_in, recv_in, send_sc, recv_sc,
+    far_proj=None, far_lists=None, proj_send=None, proj_recv=None, lists_send=None, lists_recv=None,
 ):
     dom, sub = lax.axis_index("dom"), lax.axis_index("sub")
     peers = n_dom * n_sub
@@ -58,15 +59,15 @@
         proj[:, v:v + wide] = (part * inv[:, v:v + wide]).astype(proj.dtype)
     pl.semaphore_wait(barrier, peers - 1)
 
-    def pick(k, table):
-        slot_rows = []
-        for each in (k, k + 1):
-            to_dom, to_sub = target(each)
-            slot_rows.append(lists[pl.ds(to_dom * n_sub + to_sub, 1), :])
-        slots = jnp.concatenate(slot_rows, axis=1)
+    def pick_for(first, second, table, lists):
+        slots = jnp.concatenate([lists[pl.ds(first, 1), :], lists[pl.ds(second, 1), :]], axis=1)
         hot = lax.broadcasted_iota(jnp.int32, (verts, 2 * blk), 0) == slots
         hot = jnp.where(hot, 1.0, 0.0).astype(table.dtype)
         return jnp.dot(table[...], hot, preferred_element_type=jnp.float32).astype(table.dtype)
+
+    def pick(k, table):
+        index = [to_dom * n_sub + to_sub for to_dom, to_sub in (target(k), target(k + 1))]
+        return pick_for(*index, table, lists)
 
     def deliver(table, outgoing, got, sends, recvs):
         first = pick(0, table)
@@ -98,9 +99,12 @@
             span = slice(r * blk, (r + 2) * blk)
             acc[:, span] = term if fresh else acc[:, span] + term
 
-    def aggregate(table, outgoing, got, sends, recvs, acc):
+    def add_own(table, acc):
         for c in range(0, own, 2):
             add(acc, table[:, c * blk:(c + 2) * blk], c, c + 1, c == 0)
+
+    def aggregate(table, outgoing, got, sends, recvs, acc):
+        add_own(table, acc)
 
         def arrived(k):
             block = jnp.concatenate([got[k], got[k + 1]], axis=1)
@@ -116,12 +120,107 @@
             copy(outgoing, got, sends, recvs, k + 1).wait_recv()
             arrived(k)
 
-    deliver(proj, out_in, got_in, send_in, recv_in)
+    relay = far_proj is not None
+    if relay:
+        half = lax.div(sub, 2)
+        sibling, near, far = 1 + 4 * half - sub, 2 - half, 3 - 3 * half
+        middle = sub == 1 + half
+        mine = dom * n_sub + sub
+        per_step = 2 * n_dom
+
+        def to_slot(j, source_index, to_dom, to_sub):
+            return pltpu.make_async_remote_copy(
+                src_ref=out_in.at[j], dst_ref=got_in.at[source_index], send_sem=send_in.at[j],
+                recv_sem=recv_in.at[source_index], device_id=(to_dom, to_sub), device_id_type=MESH,
+            )
+
+        def block_copies(slot):
+            return [
+                pltpu.make_async_remote_copy(
+                    src_ref=src, dst_ref=dst.at[slot], send_sem=sent, recv_sem=came.at[slot],
+                    device_id=(dom, near), device_id_type=MESH,
+                )
+                for src, dst, sent, came in (
+                    (proj, far_proj, proj_send, proj_recv), (lists, far_lists, lists_send, lists_recv)
+                )
+            ]
+
+        def send_block(slot):
+            for each in block_copies(slot):
+                each.start()
+
+        def hand_out(table, lists, source_index, base):
+            def picked_for(a):
+                row = flip(a) * n_sub
+                return pick_for(row + sub, row + sibling, table, lists)
+
+            first = picked_for(0)
+            got_in[source_index] = first[:, :blk]
+            out_in[base + 1] = first[:, blk:]
+            to_slot(base + 1, source_index, dom, sibling).start()
+
+            @pl.loop(1, n_dom)
+            def _(a):
+                picked = picked_for(a)
+                j = base + 2 * a
+                out_in[j] = picked[:, :blk]
+                out_in[j + 1] = picked[:, blk:]
+                to_slot(j + 1, source_index, flip(a), sibling).start()
+                to_slot(j, source_index, flip(a), sub).start()
+
+        def relay_block(slot, from_sub):
+            for each in block_copies(slot):
+                each.wait_recv()
+            hand_out(
+                far_proj.at[slot], far_lists.at[slot], dom * n_sub + from_sub, (slot + 1) * per_step
+            )
+
+        def wait_for(index):
+            to_slot(0, index, dom, sibling).wait_recv()
+
+        def add_pair(e0, e1):
+            block = jnp.concatenate([got_in[e0], got_in[e1]], axis=1)
+            add(acc_in, block, own + e0, own + e1, False)
+
+        pl.when(middle)(lambda: send_block(0))
+        hand_out(proj, lists, mine, 0)
+        pl.when(jnp.logical_not(middle))(lambda: send_block(1))
+    else:
+        deliver(proj, out_in, got_in, send_in, recv_in)
     w_pad[...] = jnp.zeros_like(w_pad)
     w_pad[0:classes, :] = w_outer[...]
     bias_col = jnp.broadcast_to(bias[...], (blk, hid)).T
     tile_copy.wait()
-    aggregate(proj, out_in, got_in, send_in, recv_in, acc_in)
+    if relay:
+        add_own(proj, acc_in)
+        pl.when(middle)(lambda: relay_block(0, near))
+        wait_for(dom * n_sub + sibling)
+        add_pair(mine, dom * n_sub + sibling)
+
+        @pl.loop(1, n_dom)
+        def _(a):
+            row = flip(a) * n_sub
+            wait_for(row + sub)
+            wait_for(row + sibling)
+            add_pair(row + sub, row + sibling)
+
+        pl.when(middle)(lambda: relay_block(1, far))
+        for plane in (near, far):
+            @pl.when(jnp.logical_not(middle))
+            def _():
+                wait_for(dom * n_sub + plane)
+
+            wait_for(flip(1) * n_sub + plane)
+            add_pair(dom * n_sub + plane, flip(1) * n_sub + plane)
+
+            @pl.loop(1, n_dom // 2)
+            def _(pair):
+                e0, e1 = flip(2 * pair) * n_sub + plane, flip(2 * pair + 1) * n_sub + plane
+                wait_for(e0)
+                wait_for(e1)
+                add_pair(e0, e1)
+    else:
+        aggregate(proj, out_in, got_in, send_in, recv_in, acc_in)
     for v in range(0, verts, blk):
         span = slice(v, v + blk)
         scale = inv[:, span]
@@ -135,8 +234,26 @@
 
     @pl.loop(1, peers)
     def _(k):
-        copy(out_in, got_in, send_in, recv_in, k).wait_send()
         copy(out_sc, got_sc, send_sc, recv_sc, k).wait_send()
+
+    if relay:
+        for each in block_copies(0):
+            each.wait_send()
+
+        @pl.loop(1, per_step)
+        def _(j):
+            to_slot(j, 0, dom, sibling).wait_send()
+
+        @pl.when(middle)
+        def _():
+            @pl.loop(1, per_step)
+            def _(j):
+                to_slot(per_step + j, 0, dom, sibling).wait_send()
+                to_slot(2 * per_step + j, 0, dom, sibling).wait_send()
+    else:
+        @pl.loop(1, peers)
+        def _(k):
+            copy(out_in, got_in, send_in, recv_in, k).wait_send()
 
 
 def on_device(
@@ -152,6 +269,8 @@
     order = jnp.arange(tiles.shape[1], dtype=jnp.int32)
     hit = tile_col[:, None, :] == jnp.arange(columns, dtype=jnp.int32)[None, :, None]
     where_tile = jnp.max(jnp.where(hit, order, -1), axis=2)
+    relay = n_sub == 4
+    lists_out = 6 * n_dom if relay else peers
     vmem = pl.BlockSpec(memory_space=pltpu.VMEM)
     bf16, f32 = jnp.bfloat16, jnp.float32
     agg = pl.pallas_call(
@@ -162,7 +281,7 @@
         out_specs=vmem,
         scratch_shapes=[
             pltpu.VMEM((hid, verts), bf16),
-            pltpu.VMEM((peers, hid, blk), bf16),
+            pltpu.VMEM((lists_out, hid, blk), bf16),
             pltpu.VMEM((peers, hid, blk), bf16),
             pltpu.VMEM((hid, verts), f32),
             pltpu.VMEM((padded, hid), bf16),
@@ -172,11 +291,23 @@
             pltpu.VMEM((padded, verts), f32),
             pltpu.VMEM(tiles.shape, bf16),
             pltpu.SemaphoreType.DMA,
+            pltpu.SemaphoreType.DMA((lists_out,)),
             pltpu.SemaphoreType.DMA((peers,)),
             pltpu.SemaphoreType.DMA((peers,)),
             pltpu.SemaphoreType.DMA((peers,)),
-            pltpu.SemaphoreType.DMA((peers,)),
-        ],
+        ]
+        + (
+            [
+                pltpu.VMEM((2, hid, verts), bf16),
+                pltpu.VMEM((2, peers, blk), jnp.int32),
+                pltpu.SemaphoreType.DMA,
+                pltpu.SemaphoreType.DMA((2,)),
+                pltpu.SemaphoreType.DMA,
+                pltpu.SemaphoreType.DMA((2,)),
+            ]
+            if relay
+            else []
+        ),
         compiler_params=pltpu.CompilerParams(
             collective_id=0, has_side_effects=True, vmem_limit_bytes=56 * 1024 * 1024
         ),

time: 74.7 us -> 69.6 us (0.932)
  Pallas kernels: 71.3 us -> 66.3 us
    pallas_call x1, Pallas kernels: 71.3 us -> 66.3 us  [on_device(): pl.pallas_call(functools.partial(kernel, n_dom, n_sub), out_shape=jax.Sha...]
where the time goes in v2:
time: 69.6 us; the launch traced here: 69.4 us
  Pallas kernels  66.3 us (95%)
  other arithmetic  3.11 us (4%)
    pallas_call x1, Pallas kernels, on_device(): pl.pallas_call(functools.partial(kernel, n_dom, n_sub), out_shape=jax.Sha...  66.3 us
    add x1, other arithmetic, on_device(): return inv_sqrt * agg.T + bias_outer  1.69 us
    reduce_max x1, other arithmetic, on_device(): where_tile = jnp.max(jnp.where(hit, order, -1), axis=2)  1.42 us

profile of v2, /device:TPU:0, one launch (start us, length us, event | category | flops | bytes accessed | tf_op | source)
XLA Modules:
  0.0 69.4 jit_solution(10936867918768505808)
XLA Ops:
  0.0 0.0 copy-start
  0.0 0.0 copy-start.1
  0.0 1.4 %select_reduce_fusion.where_tile = s32[8,40]{1,0:T(8,128)} fusion(s32[8,32]{1,0:T(8,128)} %param.15), kind=kLoop, calls=%fused_computation.1 | loop fusion | flops 30400 | bytes 2304 | tf_op jit(solution)/shard_map/reduce_max | solution.py:271
  1.4 66.3 %shard_map.91 = f32[41,1024]{1,0:T(8,128)} custom-call(bf16[602,1024]{1,0:T(8,128)(2,1)} %bitcast.7, bf16[602,256]{1,0:T(8,128)(2,1)} %w_inner.1, f32[1,256]{1,0:T(1,128)} %bitcast.11, bf16[41,256]{1,0:T(8,128)(2,1)} %bitcast.8, s32[1,1024]{1,0:T(1,128)} %bitcast.10, s32[32,128]{1,0:T(8,128)} %bitcast.9, s32[8,40]{1,0:T(8,128)} %select_reduce_fusion.where_tile, ...), custom_call_target="tpu_custom_call" | custom-call | tf_op jit(solution)/shard_map/pallas_call | solution.py:276
  67.7 0.0 copy-done
  67.7 0.0 copy-done.1
  67.7 1.7 %add_bitcast_fusion = f32[1024,41]{0,1:T(8,128)} fusion(f32[41,1024]{1,0:T(8,128)} %shard_map.91, f32[41]{0:T(128)S(1)} %copy-done.1, f32[1024]{0:T(1024)S(1)} %convert_rsqrt_fusion), kind=kLoop, calls=%fused_computation | loop fusion | flops 83968 | bytes 340132 | tf_op jit(solution)/shard_map/add | solution.py:319
  (1 shorter events, 0.0 us)
Async XLA Ops:
  0.0 67.7 %copy-start = (s32[1024]{0:T(1024)S(1)}, s32[1024]{0:T(1024)}, u32[]{:S(2)}) copy-start(s32[1024]{0:T(1024)} %param.16) | copy-start | bytes 12292
  0.0 67.7 %copy-start.1 = (f32[41]{0:T(128)S(1)}, f32[41]{0:T(128)}, u32[]{:S(2)}) copy-start(f32[41]{0:T(128)} %param.13) | copy-start | bytes 496

commit v3 on v2

--- a/solution.py
+++ b/solution.py
@@ -12,11 +12,19 @@
 
 
 def kernel(
-    n_dom, n_sub, ft, w_inner, bias, w_outer, degrees, lists, where_tile, tiles_hbm, out,
+    n_dom, n_sub, *refs,
+):
+    hbm, (tiles_hbm, out), staged, refs = refs[:7], refs[7:9], refs[9:16], refs[16:]
+    run(n_dom, n_sub, hbm, staged, tiles_hbm, out, *refs)
+
+
+def run(
+    n_dom, n_sub, hbm, staged, tiles_hbm, out, stage_sem, found, where_tile, found_sem,
     proj, out_in, got_in, acc_in, w_pad, scores, out_sc, got_sc, acc_sc, tiles,
     tile_sem, send_in, recv_in, send_sc, recv_sc,
     far_proj=None, far_lists=None, proj_send=None, proj_recv=None, lists_send=None, lists_recv=None,
 ):
+    ft, w_inner, bias, w_outer, degrees, lists, tile_col = staged
     dom, sub = lax.axis_index("dom"), lax.axis_index("sub")
     peers = n_dom * n_sub
     hid, verts = proj.shape
@@ -49,14 +57,29 @@
     def _(k):
         pl.semaphore_signal(barrier, inc=1, device_id=target(k), device_id_type=MESH)
 
+    staging = [
+        pltpu.make_async_copy(src, dst, stage_sem.at[i]) for i, (src, dst) in enumerate(zip(hbm, staged))
+    ]
+    for each in staging:
+        each.start()
     tile_copy = pltpu.make_async_copy(tiles_hbm, tiles, tile_sem)
     tile_copy.start()
+    for each in staging:
+        each.wait()
     inv = lax.rsqrt(degrees[...].astype(jnp.float32))
     w_t = w_inner[...].T
     wide = 2 * blk
     for v in range(0, verts, wide):
         part = jnp.dot(w_t, ft[:, v:v + wide], preferred_element_type=jnp.float32)
         proj[:, v:v + wide] = (part * inv[:, v:v + wide]).astype(proj.dtype)
+    cols = tile_col[...]
+    lane = lax.broadcasted_iota(jnp.int32, found.shape, 1)
+    place = jnp.full(found.shape, -1, jnp.int32)
+    for t in range(per_row):
+        place = jnp.where(cols[:, t:t + 1] == lane, t, place)
+    found[...] = place
+    found_copy = pltpu.make_async_copy(found, where_tile, found_sem)
+    found_copy.start()
     pl.semaphore_wait(barrier, peers - 1)
 
     def pick_for(first, second, table, lists):
@@ -127,6 +150,7 @@
         middle = sub == 1 + half
         mine = dom * n_sub + sub
         per_step = 2 * n_dom
+        direct = 2
 
         def to_slot(j, source_index, to_dom, to_sub):
             return pltpu.make_async_remote_copy(
@@ -149,17 +173,21 @@
             for each in block_copies(slot):
                 each.start()
 
-        def hand_out(table, lists, source_index, base):
+        def hand_out(table, lists, source_index, base, skip):
             def picked_for(a):
                 row = flip(a) * n_sub
                 return pick_for(row + sub, row + sibling, table, lists)
 
             first = picked_for(0)
             got_in[source_index] = first[:, :blk]
-            out_in[base + 1] = first[:, blk:]
-            to_slot(base + 1, source_index, dom, sibling).start()
-
-            @pl.loop(1, n_dom)
+            if skip == 0:
+                out_in[base + 1] = first[:, blk:]
+                to_slot(base + 1, source_index, dom, sibling).start()
+            for a in range(1, skip):
+                out_in[base + 2 * a] = picked_for(a)[:, :blk]
+                to_slot(base + 2 * a, source_index, flip(a), sub).start()
+
+            @pl.loop(max(1, skip), n_dom)
             def _(a):
                 picked = picked_for(a)
                 j = base + 2 * a
@@ -172,8 +200,17 @@
             for each in block_copies(slot):
                 each.wait_recv()
             hand_out(
-                far_proj.at[slot], far_lists.at[slot], dom * n_sub + from_sub, (slot + 1) * per_step
+                far_proj.at[slot], far_lists.at[slot], dom * n_sub + from_sub, (slot + 1) * per_step,
+                direct,
             )
+
+        def send_direct():
+            rows_for = [flip(a) * n_sub + far for a in range(2)]
+            picked = pick_for(*rows_for, proj, lists)
+            for a in range(2):
+                j = per_step + 2 * a + 1
+                out_in[j] = picked[:, a * blk:(a + 1) * blk]
+                to_slot(j, mine, flip(a), far).start()
 
         def wait_for(index):
             to_slot(0, index, dom, sibling).wait_recv()
@@ -183,14 +220,16 @@
             add(acc_in, block, own + e0, own + e1, False)
 
         pl.when(middle)(lambda: send_block(0))
-        hand_out(proj, lists, mine, 0)
+        hand_out(proj, lists, mine, 0, 0)
         pl.when(jnp.logical_not(middle))(lambda: send_block(1))
+        send_direct()
     else:
         deliver(proj, out_in, got_in, send_in, recv_in)
     w_pad[...] = jnp.zeros_like(w_pad)
     w_pad[0:classes, :] = w_outer[...]
     bias_col = jnp.broadcast_to(bias[...], (blk, hid)).T
     tile_copy.wait()
+    found_copy.wait()
     if relay:
         add_own(proj, acc_in)
         pl.when(middle)(lambda: relay_block(0, near))
@@ -244,9 +283,16 @@
         def _(j):
             to_slot(j, 0, dom, sibling).wait_send()
 
+        for a in range(direct):
+            to_slot(per_step + 2 * a + 1, 0, dom, sibling).wait_send()
+
         @pl.when(middle)
         def _():
-            @pl.loop(1, per_step)
+            for base in (per_step, 2 * per_step):
+                for a in range(1, direct):
+                    to_slot(base + 2 * a, 0, dom, sibling).wait_send()
+
+            @pl.loop(2 * direct, per_step)
             def _(j):
                 to_slot(per_step + j, 0, dom, sibling).wait_send()
                 to_slot(2 * per_step + j, 0, dom, sibling).wait_send()
@@ -266,9 +312,10 @@
     padded = 16 * ((classes + 15) // 16)
     blk = tiles.shape[2]
     columns = verts // blk + peers
-    order = jnp.arange(tiles.shape[1], dtype=jnp.int32)
-    hit = tile_col[:, None, :] == jnp.arange(columns, dtype=jnp.int32)[None, :, None]
-    where_tile = jnp.max(jnp.where(hit, order, -1), axis=2)
+    lanes = 128 * ((columns + 127) // 128)
+    small = (
+        features.T, w_inner, bias_inner[None, :], w_outer.T, degrees[None, :], send_rows[0], tile_col
+    )
     relay = n_sub == 4
     lists_out = 6 * n_dom if relay else peers
     vmem = pl.BlockSpec(memory_space=pltpu.VMEM)
@@ -276,10 +323,14 @@
     agg = pl.pallas_call(
         functools.partial(kernel, n_dom, n_sub),
         out_shape=jax.ShapeDtypeStruct((classes, verts), f32),
-        in_specs=[vmem] * 6
-        + [pl.BlockSpec(memory_space=pltpu.SMEM), pl.BlockSpec(memory_space=pl.ANY)],
+        in_specs=[pl.BlockSpec(memory_space=pl.ANY)] * 8,
         out_specs=vmem,
-        scratch_shapes=[
+        scratch_shapes=[pltpu.VMEM(each.shape, each.dtype) for each in small]
+        + [
+            pltpu.SemaphoreType.DMA((7,)),
+            pltpu.VMEM((tiles.shape[0], lanes), jnp.int32),
+            pltpu.SMEM((tiles.shape[0], lanes), jnp.int32),
+            pltpu.SemaphoreType.DMA,
             pltpu.VMEM((hid, verts), bf16),
             pltpu.VMEM((lists_out, hid, blk), bf16),
             pltpu.VMEM((peers, hid, blk), bf16),
@@ -311,10 +362,7 @@
         compiler_params=pltpu.CompilerParams(
             collective_id=0, has_side_effects=True, vmem_limit_bytes=56 * 1024 * 1024
         ),
-    )(
-        features.T, w_inner, bias_inner[None, :], w_outer.T, degrees[None, :], send_rows[0],
-        where_tile, tiles,
-    )
+    )(*small, tiles)
     inv_sqrt = lax.rsqrt(degrees.astype(f32))[:, None]
     return inv_sqrt * agg.T + bias_outer
 

time: 69.6 us -> 66.1 us (0.950)
  Pallas kernels: 66.3 us -> 63.5 us
  other arithmetic: 3.11 us -> 2.39 us
    pallas_call x1, Pallas kernels: 66.3 us -> 63.5 us  [on_device(): pl.pallas_call(functools.partial(kernel, n_dom, n_sub), out_shape=jax.Sha...]
    reduce_max x1 -> x0, other arithmetic: 1.42 us -> none  [on_device(): where_tile = jnp.max(jnp.where(hit, order, -1), axis=2)]
    rsqrt x1, other arithmetic: 0.01 us -> 0.7 us  [on_device(): inv_sqrt = lax.rsqrt(degrees.astype(f32))[:, None]]
where the time goes in v3:
time: 66.1 us; the launch traced here: 65.9 us
  Pallas kernels  63.5 us (96%)
  other arithmetic  2.39 us (4%)
    pallas_call x1, Pallas kernels, on_device(): pl.pallas_call(functools.partial(kernel, n_dom, n_sub), out_shape=jax.Sha...  63.5 us
    add x1, other arithmetic, on_device(): return inv_sqrt * agg.T + bias_outer  1.69 us

profile of v3, /device:TPU:0, one launch (start us, length us, event | category | flops | bytes accessed | tf_op | source)
XLA Modules:
  0.0 65.9 jit_solution(13985689865801838480)
XLA Ops:
  0.0 0.0 copy-start
  0.0 0.7 %convert_rsqrt_fusion = f32[1024]{0:T(1024)S(1)} fusion(s32[1024]{0:T(1024)} %param.16), kind=kLoop, calls=%fused_computation.1 | loop fusion | flops 1024 | bytes 8192 | tf_op jit(solution)/shard_map/rsqrt | solution.py:366
  0.7 63.5 %shard_map.91 = f32[41,1024]{1,0:T(8,128)} custom-call(bf16[602,1024]{1,0:T(8,128)(2,1)} %bitcast.7, bf16[602,256]{1,0:T(8,128)(2,1)} %refs_1_.1, f32[1,256]{1,0:T(1,128)} %bitcast.11, bf16[41,256]{1,0:T(8,128)(2,1)} %bitcast.8, s32[1,1024]{1,0:T(1,128)} %bitcast.10, s32[32,128]{1,0:T(8,128)} %bitcast.9, s32[8,32]{1,0:T(8,128)} %refs_6_.1, ...), custom_call_target="tpu_custom_call" | custom-call | tf_op jit(solution)/shard_map/pallas_call | solution.py:323
  64.2 0.0 copy-done
  64.2 1.7 %add_bitcast_fusion = f32[1024,41]{0,1:T(8,128)} fusion(f32[41,1024]{1,0:T(8,128)} %shard_map.91, f32[41]{0:T(128)S(1)} %copy-done, f32[1024]{0:T(1024)S(1)} %convert_rsqrt_fusion), kind=kLoop, calls=%fused_computation | loop fusion | flops 83968 | bytes 340132 | tf_op jit(solution)/shard_map/add | solution.py:367
Async XLA Ops:
  0.0 64.2 %copy-start = (f32[41]{0:T(128)S(1)}, f32[41]{0:T(128)}, u32[]{:S(2)}) copy-start(f32[41]{0:T(128)} %param.13) | copy-start | bytes 496
